TPU v7x, 32 devices: a whole 2x2x4 slice. The times are simulated.
32 devices in a mesh: dev: 16 (over z, y, x), rep: 2 (over core).
Axes of the slice: x: 2, y: 2, z: 4, core: 2. Of those that a mesh axis runs over, the one named last changes fastest.
Arguments:
- embeddings: float32 [4096, 4096], P(('rep', 'dev')), parts along dimension 0, may hold values from -130 to 130
- cluster_id: int32 [4096], P(('rep', 'dev')), parts along dimension 0, may hold values from 0 to 31, as said below
- member_order: int32 [4096], P(('rep', 'dev')), parts along dimension 0, may hold values from 0 to 127, as said below
- cluster_slot: int32 [64], P('rep'), parts along dimension 0, may hold values from 0 to 31, each once
- cluster_size: int32 [64], P('rep'), parts along dimension 0, may hold values from 16 to 128, as said below
Outputs:
- best_similarity: float32 [4096], P(('rep', 'dev')), parts along dimension 0
- keep: int32 [4096], P(('rep', 'dev')), parts along dimension 0
- cluster_mean: float32 [64], P(('rep', 'dev')), parts along dimension 0
There are 2 independent parts, one for each index of `rep`. A program takes and returns all parts, laid end to end along the dimension named above; each array names one. Nothing has to cross between parts.
Inputs may be any that keep to these rules, and one draw needn't show every extreme that they name: `cluster_id`: every cluster holds at most 128 rows and some cluster exactly 128. A cluster of n members has floor(n / 16) or ceil(n / 16) of them among the rows of each device, so at most 8, a number reached on every device. `member_order`: within a cluster of n members the ranks are 0 to n - 1, each once. `cluster_slot`: a permutation; cluster c is owned by device cluster_slot[c] // 2 of dev. `cluster_size`: the number of rows whose cluster_id is c.
All inputs are finite; a program needn't handle non-finite values.
Results may differ from a plain program's by a relative error of at most 0.0003.
Values may be sent and summed in bfloat16 or wider, within the bound.
A program may use at most 64 MiB of HBM per device.

v0:
```python
import jax
import jax.numpy as jnp
from jax import lax
from jax.sharding import PartitionSpec as P

CAP = 128


norm_eps = 1e-06
cutoff = 0.8


def normalized(values):
    squares_sum = jnp.sum(values * values, axis=1, keepdims=True)
    return (values * lax.rsqrt(squares_sum + norm_eps)).astype(jnp.bfloat16)


def block_best(row_units, col_units, is_live):
    similar = jnp.einsum("cid,cjd->cij", row_units, col_units, preferred_element_type=jnp.float32)
    count_rows = row_units.shape[1]
    count_cols = col_units.shape[1]
    row_pos = lax.broadcasted_iota(jnp.int32, (count_rows, count_cols), 0)
    col_pos = lax.broadcasted_iota(jnp.int32, (count_rows, count_cols), 1)
    allowed = (col_pos < row_pos)[None] & is_live[:, None, :count_cols]
    return jnp.max(jnp.where(allowed, similar, -1.0), axis=2)


def body(embeddings, cluster_id, member_order, cluster_slot, cluster_size):
    devices = lax.axis_size("dev")
    clusters = cluster_slot.shape[0]
    per_owner = clusters // devices
    row_count = embeddings.shape[0]
    capacity = CAP
    per_pair = capacity // devices
    columns = lax.broadcasted_iota(jnp.int32, (row_count, clusters), 1)
    member = cluster_id[:, None] == columns
    slot_row = jnp.sum(jnp.where(member, cluster_slot[None, :], 0), axis=1)
    earlier = (
        lax.broadcasted_iota(jnp.int32, (row_count, row_count), 1)
        < lax.broadcasted_iota(jnp.int32, (row_count, row_count), 0)
    ).astype(jnp.bfloat16)
    before = jnp.dot(earlier, member.astype(jnp.bfloat16), preferred_element_type=jnp.float32)
    row_rank = jnp.sum(jnp.where(member, before, 0.0), axis=1).astype(jnp.int32)
    send_place = slot_row * per_pair + row_rank
    source_row = (
        jnp.zeros((clusters * per_pair,), jnp.int32)
        .at[send_place]
        .set(jnp.arange(row_count, dtype=jnp.int32) + 1)
    )
    filled = source_row > 0
    row_pick = jnp.maximum(source_row - 1, 0)
    sent_order = jnp.where(filled, member_order[row_pick], -1)
    payload = normalized(embeddings)[row_pick]
    got_rows, got_order = (
        lax.all_to_all(payload, "dev", split_axis=0, concat_axis=0, tiled=True),
        lax.all_to_all(sent_order, "dev", split_axis=0, concat_axis=0, tiled=True),
    )
    slots_in = got_order.shape[0]
    local_cluster = jnp.arange(slots_in, dtype=jnp.int32) // per_pair % per_owner
    is_valid = got_order >= 0
    position = jnp.where(is_valid, local_cluster * capacity + got_order, per_owner * capacity)
    arrival = (
        jnp.zeros((per_owner * capacity,), jnp.int32)
        .at[position]
        .set(jnp.arange(slots_in, dtype=jnp.int32) + 1, mode="drop")
    )
    occupied = arrival > 0
    gathered = got_rows[jnp.maximum(arrival - 1, 0)]
    unit_rows = jnp.where(occupied[:, None], gathered, jnp.zeros((), jnp.bfloat16))
    unit_rows = unit_rows.reshape(per_owner, capacity, unit_rows.shape[1])
    owner_index = lax.axis_index("dev")
    my_slots = owner_index * per_owner + jnp.arange(per_owner, dtype=jnp.int32)
    own_match = cluster_slot[None, :] == my_slots[:, None]
    my_size = jnp.sum(jnp.where(own_match, cluster_size[None, :], 0), axis=1)
    spot_index = lax.broadcasted_iota(jnp.int32, (per_owner, capacity), 1)
    is_live = occupied.reshape(per_owner, capacity) & (spot_index < my_size[:, None])
    nearest = block_best(unit_rows, unit_rows, is_live)
    best_spot = jnp.where(is_live, nearest, -1.0)
    cluster_mean = jnp.sum(jnp.where(is_live, best_spot, 0.0), axis=1) / my_size.astype(jnp.float32)
    flat_best = best_spot.reshape(-1)
    answer = jnp.where(is_valid, flat_best[jnp.minimum(position, per_owner * capacity - 1)], 0.0)
    returned = lax.all_to_all(answer, "dev", split_axis=0, concat_axis=0, tiled=True)
    row_best = returned[send_place]
    keep_mask = (row_best < cutoff).astype(jnp.int32)
    return (row_best, keep_mask, cluster_mean)


def solution(mesh):
    placed = (P(("rep", "dev"), None), P(("rep", "dev")), P(("rep", "dev")), P("rep"), P("rep"))
    return jax.shard_map(
        body,
        mesh=mesh,
        in_specs=placed,
        out_specs=(P(("rep", "dev")), P(("rep", "dev")), P(("rep", "dev"))),
        check_vma=False,
    )
```

profile of v0, /device:TPU:0, one launch (start us, length us, event | category | flops | bytes accessed | tf_op | source)
XLA Modules:
  0.0 98.7 jit_solution(10405978561421761780)
XLA Ops:
  0.6 0.0 copy-start
  0.6 0.0 copy-start.1
  0.7 1.0 fusion.9
  1.6 0.8 select_reduce_fusion
  2.4 1.0 scatter_custom_fusion
  3.4 0.0 copy-done
  3.4 1.9 %gather_fusion = s32[256]{0:T(256)S(1)} fusion(s32[128]{0:T(128)S(1)} %copy-done, s32[1024]{0:T(1024)S(1)} %pad_clamp_fusion.3), kind=kCustom, calls=%fused_computation | custom fusion | bytes 3072 | tf_op jit(solution)/shard_map/gather | solution.py:52
  5.3 0.7 all_to_all.22
  6.0 8.3 %all-to-all-start = ((s32[16,16,1]{1,2,0:T(1,128)}), s32[16,16,1]{1,2,0:T(1,128)S(1)}, u32[]{:S(2)}, u32[]{:S(2)}) async-start(s32[16,16,1]{1,2,0:T(1,128)} %bitcast.2), calls=%async_computation | async-start | bytes 16384 | tf_op jit(solution)/shard_map/all_to_all | solution.py:56
  14.3 1.8 %multiply_reduce_fusion = f32[128]{0:T(128)S(1)} fusion(f32[128,4096]{1,0:T(8,128)} %param.5), kind=kLoop, calls=%fused_computation.10 | loop fusion | flops 1048448 | bytes 2097664 | tf_op jit(solution)/shard_map/reduce_sum | solution.py:14
  16.2 0.0 copy-done.1
  16.2 0.2 multiply_convert_fusion
  16.4 3.2 %gather_fusion.1 = bf16[256,4096]{1,0:T(8,128)(2,1)} fusion(bf16[128,4096]{1,0:T(8,128)(2,1)S(1)} %multiply_convert_fusion, s32[1024]{0:T(1024)S(1)} %pad_clamp_fusion.3), kind=kCustom, calls=%fused_computation.1 | custom fusion | bytes 4195328 | tf_op jit(solution)/shard_map/gather | solution.py:53
  19.6 2.0 %all-to-all-done = s32[16,16,1]{1,2,0:T(1,128)S(1)} async-done(((s32[16,16,1]{1,2,0:T(1,128)}), s32[16,16,1]{1,2,0:T(1,128)S(1)}, u32[]{:S(2)}, u32[]{:S(2)}) %all-to-all-start) | async-done | bytes 1056 | tf_op jit(solution)/shard_map/all_to_all | solution.py:56
  21.6 0.0 copy-start.2
  21.6 0.0 copy-start.3
  21.6 5.0 %all-to-all-start.1 = ((bf16[16,16,4096]{2,1,0:T(8,128)(2,1)}), bf16[16,16,4096]{2,1,0:T(8,128)(2,1)S(1)}, u32[]{:S(2)}, u32[]{:S(2)}) async-start(bf16[16,16,4096]{2,1,0:T(8,128)(2,1)} %bitcast.24), calls=%async_computation.1 | async-start | bytes 4194304 | tf_op jit(solution)/shard_map/all_to_all | solution.py:55
  26.7 0.0 copy-done.2
  26.7 0.0 copy-done.3
  26.7 0.2 fusion.14
  26.9 0.5 broadcast.330
  27.4 0.7 reduce.6
  28.1 0.1 all_to_all.24
  28.2 1.4 %scatter_custom_fusion.1 = s32[256]{0:T(256)S(1)} fusion(s32[256]{0:T(256)S(1)} %bitcast.28, s32[256]{0:T(256)S(1)} %iota_add_fusion, s32[]{:T(128)} %constant.28.clone.1), kind=kCustom, calls=%fused_computation.59 | custom fusion | bytes 1028 | tf_op jit(solution)/shard_map/scatter | solution.py:65
  29.7 0.1 fusion.18
  29.8 39.6 %all-to-all-done.1 = bf16[16,16,4096]{2,1,0:T(8,128)(2,1)S(1)} async-done(((bf16[16,16,4096]{2,1,0:T(8,128)(2,1)}), bf16[16,16,4096]{2,1,0:T(8,128)(2,1)S(1)}, u32[]{:S(2)}, u32[]{:S(2)}) %all-to-all-start.1) | async-done | bytes 2097184 | tf_op jit(solution)/shard_map/all_to_all | solution.py:55
  69.4 3.2 %gather_fusion.2 = bf16[256,4096]{1,0:T(8,128)(2,1)} fusion(bf16[256,4096]{1,0:T(8,128)(2,1)S(1)} %bitcast.23, s32[1024]{0:T(1024)S(1)} %pad_clamp_fusion.2), kind=kCustom, calls=%fused_computation.2 | custom fusion | bytes 4195328 | tf_op jit(solution)/shard_map/gather | solution.py:68
  72.6 3.0 %fusion.6 = f32[2,128]{1,0:T(2,128)S(1)} fusion(bf16[2,128,4096]{2,1,0:T(8,128)(2,1)} %bitcast.25, pred[2,128]{1,0:T(4,128)(4,1)S(1)} %get-tuple-element.6, pred[2,128]{1,0:T(4,128)(4,1)S(1)} %get-tuple-element.5, pred[128,128]{0,1:T(8,128)(4,1)S(1)} %iota_compare_fusion), kind=kOutput, calls=%fused_computation.13 | convolution fusion | flops 269582080 | bytes 2115072 | tf_op jit(solution)/shard_map/cid,cjd->cij/dot_general | solution.py:19
  75.6 0.1 fusion.12
  75.7 0.1 fusion.13
  75.8 2.0 %gather_fusion.3 = f32[256]{0:T(256)S(1)} fusion(f32[256]{0:T(256)S(1)} %fusion.12, s32[1024]{0:T(1024)S(1)} %pad_clamp_fusion.1), kind=kCustom, calls=%fused_computation.3 | custom fusion | bytes 3072 | tf_op jit(solution)/shard_map/gather | solution.py:81
  77.8 0.1 gather.24
  77.8 0.6 compare_select_fusion
  78.4 9.8 %all-to-all-start.2 = ((f32[16,16,1]{1,2,0:T(1,128)}), f32[16,16,1]{1,2,0:T(1,128)S(1)}, u32[]{:S(2)}, u32[]{:S(2)}) async-start(f32[16,16,1]{1,2,0:T(1,128)} %bitcast.12), calls=%async_computation.2 | async-start | bytes 16384 | tf_op jit(solution)/shard_map/all_to_all | solution.py:82
  88.3 0.5 convert_divide_fusion
  88.8 6.8 %all-to-all-done.2 = f32[16,16,1]{1,2,0:T(1,128)S(1)} async-done(((f32[16,16,1]{1,2,0:T(1,128)}), f32[16,16,1]{1,2,0:T(1,128)S(1)}, u32[]{:S(2)}, u32[]{:S(2)}) %all-to-all-start.2) | async-done | bytes 1056 | tf_op jit(solution)/shard_map/all_to_all | solution.py:82
  95.6 0.5 broadcast.331
  96.1 0.7 reduce.7
  96.8 0.1 all_to_all.29
  96.8 1.3 %gather_fusion.4 = f32[128]{0:T(128)S(1)} fusion(f32[256]{0:T(256)S(1)} %all_to_all.29, s32[1024]{0:T(1024)S(1)} %pad_clamp_fusion), kind=kCustom, calls=%fused_computation.4 | custom fusion | bytes 1536 | tf_op jit(solution)/shard_map/gather | solution.py:83
  98.1 0.0 copy-start.4
  98.1 0.5 compare_convert_fusion
  98.6 0.0 copy-done.4
  (15 shorter events, 0.1 us)
Async XLA Ops:
  0.6 2.8 %copy-start = (s32[128]{0:T(128)S(1)}, s32[128]{0:T(128)}, u32[]{:S(2)}) copy-start(s32[128]{0:T(128)} %param.7) | copy-start | bytes 1540
  0.6 15.5 %copy-start.1 = (f32[128,4096]{1,0:T(8,128)S(1)}, f32[128,4096]{1,0:T(8,128)}, u32[]{:S(2)}) copy-start(f32[128,4096]{1,0:T(8,128)} %param.5) | copy-start | bytes 6291460
  6.0 15.7 %all-to-all-start = ((s32[16,16,1]{1,2,0:T(1,128)}), s32[16,16,1]{1,2,0:T(1,128)S(1)}, u32[]{:S(2)}, u32[]{:S(2)}) async-start(s32[16,16,1]{1,2,0:T(1,128)} %bitcast.2), calls=%async_computation | async-start | bytes 16384 | tf_op jit(solution)/shard_map/all_to_all | solution.py:56
  21.6 5.1 %copy-start.2 = (s32[32]{0:T(128)S(1)}, s32[32]{0:T(128)}, u32[]{:S(2)}) copy-start(s32[32]{0:T(128)} %param.8) | copy-start | bytes 388
  21.6 5.1 %copy-start.3 = (s32[32]{0:T(128)S(1)}, s32[32]{0:T(128)}, u32[]{:S(2)}) copy-start(s32[32]{0:T(128)} %param.9) | copy-start | bytes 388
  21.6 47.7 %all-to-all-start.1 = ((bf16[16,16,4096]{2,1,0:T(8,128)(2,1)}), bf16[16,16,4096]{2,1,0:T(8,128)(2,1)S(1)}, u32[]{:S(2)}, u32[]{:S(2)}) async-start(bf16[16,16,4096]{2,1,0:T(8,128)(2,1)} %bitcast.24), calls=%async_computation.1 | async-start | bytes 4194304 | tf_op jit(solution)/shard_map/all_to_all | solution.py:55
  78.4 17.1 %all-to-all-start.2 = ((f32[16,16,1]{1,2,0:T(1,128)}), f32[16,16,1]{1,2,0:T(1,128)S(1)}, u32[]{:S(2)}, u32[]{:S(2)}) async-start(f32[16,16,1]{1,2,0:T(1,128)} %bitcast.12), calls=%async_computation.2 | async-start | bytes 16384 | tf_op jit(solution)/shard_map/all_to_all | solution.py:82
  98.1 0.5 copy-start.4
where the time goes:
time: 99 us; the launch traced here: 98.7 us
  waiting for transfers between devices  48.4 us (49%)
  starting transfers between devices  23.2 us (23%)
  local copies, waits for them, and re-layouts  15.8 us (16%)
  other arithmetic  6.33 us (6%)
  matrix products  3.99 us (4%)
    all_to_all x1, waiting for transfers between devices, body(): lax.all_to_all(payload, 'dev', split_axis=0, concat_axis=0, tiled=True)  39.6 us
    all_to_all x1, starting transfers between devices, body(): lax.all_to_all(answer, 'dev', split_axis=0, concat_axis=0, tiled=True)  9.83 us
    all_to_all x1, starting transfers between devices, body(): lax.all_to_all(sent_order, 'dev', split_axis=0, concat_axis=0, tiled=True)  8.34 us
    all_to_all x1, waiting for transfers between devices, body(): lax.all_to_all(answer, 'dev', split_axis=0, concat_axis=0, tiled=True)  6.77 us
    all_to_all x1, starting transfers between devices, body(): lax.all_to_all(payload, 'dev', split_axis=0, concat_axis=0, tiled=True)  5.01 us
    gather x1, local copies, waits for them, and re-layouts, body(): payload = normalized(embeddings)[row_pick]  3.2 us
    gather x1, local copies, waits for them, and re-layouts, body(): gathered = got_rows[jnp.maximum(arrival - 1, 0)]  3.2 us
    dot_general x1, matrix products, block_best(): jnp.einsum('cid,cjd->cij', row_units, col_units, preferred_element_type=j...  3.02 us
  transfers between devices with their start and end apart: 3, of which 3 were waited for; matrix products, arithmetic and copies ran while one was open for 9% of the time, Pallas kernels for 0%

commit v1 on v0

v1 whole, which is shorter than its diff:
```python
import functools

import jax
import jax.numpy as jnp
from jax import lax
from jax.experimental import pallas as pl
from jax.experimental.pallas import tpu as pltpu
from jax.sharding import PartitionSpec as P

CAP = 128
CHUNK = 256
NORM_EPS = 1e-06
CUTOFF = 0.8
F32 = jnp.float32
BF16 = jnp.bfloat16
I32 = jnp.int32


def split_lines(n):
    for z in range(1, n + 1):
        if n % z == 0 and z * z >= n:
            return z, n // z


def iota(shape, dim):
    return lax.broadcasted_iota(I32, shape, dim)


def rows_of(values, width):
    row = iota((8, width), 0)
    out = jnp.zeros((8, width), values[0].dtype)
    for r, v in enumerate(values):
        out = jnp.where(row == r, jnp.broadcast_to(v, (8, width)), out)
    return out


def to_col(row, count):
    eye = iota((count, count), 0) == iota((count, count), 1)
    return jnp.sum(jnp.where(eye, row, 0.0), axis=1, keepdims=True)


def floor_div(x, d):
    return jnp.floor((x + 0.5) * (1.0 / d))


def kernel(n, nz, nq, emb, cid, order, slot, size, best_out, keep_out, mean_out,
           unit, line, meta, place, pick, packed, plane, ots, otr, gram, hs, hr, table,
           s_meta, r_meta, s_line, r_line, s_plane, r_plane, s_ot, r_ot, s_h, r_h, s_t, r_t):
    me = lax.axis_index("dev")
    z, q = lax.div(me, nq), lax.rem(me, nq)
    rows = emb.shape[0]
    clusters = slot.shape[1]
    per_owner = clusters // n
    chunks, width = unit.shape[1], unit.shape[3]
    group = nz * per_owner
    seg = CAP // nq
    slots = group * seg
    half = CAP // 2

    def copy(src, dst, s, r, target):
        return pltpu.make_async_remote_copy(
            src_ref=src, dst_ref=dst, send_sem=s, recv_sem=r,
            device_id={"dev": target}, device_id_type=pl.DeviceIdType.MESH)

    def on_line(d):
        return lax.rem(z + d, nz)

    def on_plane(d):
        return lax.rem(q + d, nq)

    barrier = pltpu.get_barrier_semaphore()
    for d in range(1, n):
        pl.semaphore_signal(barrier, inc=1, device_id={"dev": lax.rem(me + d, n)},
                            device_id_type=pl.DeviceIdType.MESH)

    meta[z] = rows_of([cid[...], order[...]], rows)
    x = emb[...]
    scale = lax.rsqrt(jnp.sum(x * x, axis=1, keepdims=True) + NORM_EPS)
    pl.semaphore_wait(barrier, n - 1)

    started = []
    metas = [copy(meta.at[z], meta.at[z], s_meta.at[d], r_meta.at[d], on_line(d) * nq + q)
             for d in range(1, nz)]
    for c in metas:
        c.start()
    lines = []
    for k in range(chunks):
        for t in range(nz):
            c0 = (t * chunks + k) * width
            unit[t, k] = (emb[:, c0:c0 + width] * scale).astype(BF16)
        now = [copy(unit.at[on_line(d), k], line.at[k, z], s_line.at[k, d], r_line.at[k, d],
                    on_line(d) * nq + q) for d in range(1, nz)]
        for c in now:
            c.start()
        line[k, z] = unit[z, k]
        lines.append(now)

    slot_c = to_col(slot[...].astype(F32), clusters)
    size_c = to_col(size[...].astype(F32), clusters)
    owner_c = floor_div(slot_c, per_owner)
    local_c = slot_c - owner_c * per_owner
    oz_c = floor_div(owner_c, nq)
    oq_c = owner_c - oz_c * nq
    place_c = oq_c * slots + (oz_c * per_owner + local_c) * seg
    s8_c = owner_c * 8 + local_c
    for c in metas:
        c.wait_recv()
    tri = (iota((rows, rows), 0) < iota((rows, rows), 1)).astype(F32).astype(BF16)
    base = jnp.zeros((clusters, 1), F32)
    for b in range(nz):
        is_mem = iota((clusters, rows), 0) == meta[b, 0:1, :]
        mem = is_mem.astype(F32)
        before = base + jnp.dot(mem.astype(BF16), tri, preferred_element_type=F32)

        def of_row(v):
            return jnp.sum(jnp.where(is_mem, v, 0.0), axis=0, keepdims=True)

        rank = of_row(before)
        vals = [of_row(place_c) + rank, rank + (q * seg).astype(F32), of_row(s8_c),
                meta[b, 1:2, :].astype(F32) + 1.0]
        place[:, b * rows:(b + 1) * rows] = rows_of(vals, rows)
        base = base + jnp.sum(mem, axis=1, keepdims=True)

    all_rows = nz * rows
    place_i = place[0:1, :].astype(I32)
    key_i = (place[2:3, :] * CAP + place[1:2, :]).astype(I32)
    order_b = jnp.broadcast_to(place[3:4, :], (8, all_rows)).astype(BF16)

    def make_pick(t, _):
        hit = iota((slots, all_rows), 0) + t * slots == place_i
        pick[t] = jnp.where(hit, 1.0, 0.0).astype(BF16)
        rows_l = []
        for l in range(per_owner):
            at = ((z * nq + t) * 8 + l) * CAP
            sel = jnp.where(iota((CAP, all_rows), 0) + at == key_i, 1.0, 0.0).astype(BF16)
            r = lax.dot_general(order_b, sel, (((1,), (1,)), ((), ())), preferred_element_type=F32)
            rows_l.append(r[0:1, :])
        ots[t] = rows_of(rows_l, CAP)
        return 0

    lax.fori_loop(0, nq, make_pick, 0)
    otr[q] = ots[q]
    orders = [copy(ots.at[on_plane(d)], otr.at[q], s_ot.at[d], r_ot.at[d], z * nq + on_plane(d))
              for d in range(1, nq)]
    for c in orders:
        c.start()

    planes = []
    for k in range(chunks):
        for c in lines[k]:
            c.wait_recv()
        block = line[k].reshape(all_rows, width)
        now = []
        for d in list(range(1, nq)) + [0]:
            t = on_plane(d)
            got = jnp.dot(pick[t], block, preferred_element_type=F32).astype(BF16)
            got = got.reshape(group, seg, width)
            if d == 0:
                plane[k, q] = got
            else:
                packed[k, t] = got
                c = copy(packed.at[k, t], plane.at[k, q], s_plane.at[k, d], r_plane.at[k, d],
                         z * nq + t)
                c.start()
                now.append(c)
        planes.append(now)

    for k in range(chunks):
        for c in planes[k]:
            c.wait_recv()
        for e in range(group):
            m = plane[k, :, e].reshape(CAP, width)
            s = lax.dot_general(m, m, (((1,), (1,)), ((), ())), preferred_element_type=F32)
            if k == 0:
                gram[e] = s
            else:
                gram[e] = gram[e] + s

    below = iota((half, CAP), 0) + half > iota((half, CAP), 1)

    def pack_half(t, _):
        for l in range(per_owner):
            full = gram[t * per_owner + l]
            hs[t, l] = jnp.where(below, full[half:, :], pltpu.roll(full[:half, :], half, 1))
        return 0

    lax.fori_loop(0, nz, pack_half, 0)
    halves = [copy(hs.at[on_line(d)], hr.at[z], s_h.at[d], r_h.at[d], on_line(d) * nq + q)
              for d in range(1, nz)]
    for c in halves:
        c.start()
    hr[z] = hs[z]
    for c in orders:
        c.wait_recv()
    ord_r = otr[0]
    for t in range(1, nq):
        ord_r = ord_r + otr[t]
    ord_cols = ord_r.T
    for c in halves:
        c.wait_recv()
    bests, means = [], []
    up = iota((half, half), 0) < iota((half, half), 1)
    down = iota((half, half), 0) > iota((half, half), 1)
    for l in range(per_owner):
        p = hr[0, l]
        for t in range(1, nz):
            p = p + hr[t, l]
        pt = p.T
        u, ut = p[:, half:], pt[half:, :]
        top = jnp.concatenate([jnp.where(up, u, ut), pt[:half, :]], axis=1)
        bottom = jnp.concatenate([p[:, :half], jnp.where(down, u, ut)], axis=1)
        sim = jnp.concatenate([top, bottom], axis=0)
        mine = (me * per_owner + l).astype(F32)
        n_mem = jnp.sum(jnp.where(slot_c == mine, size_c, 0.0), axis=0, keepdims=True)
        o_row, o_col = ord_r[l:l + 1, :], ord_cols[:, l:l + 1]
        ok = (o_col < o_row) & (o_col >= 1.0) & (o_col <= n_mem)
        near = jnp.max(jnp.where(ok, sim, -1.0), axis=0, keepdims=True)
        live = (o_row >= 1.0) & (o_row <= n_mem)
        bests.append(jnp.where(live, near, -1.0))
        means.append(jnp.sum(jnp.where(live, near, 0.0), axis=1, keepdims=True) / n_mem)
    table[me] = rows_of(bests, CAP)
    backs = [copy(table.at[me], table.at[me], s_t.at[d], r_t.at[d], lax.rem(me + d, n))
             for d in range(1, n)]
    for c in backs:
        c.start()
    mean = jnp.zeros((1, per_owner), F32)
    for l in range(per_owner):
        mean = jnp.where(iota((1, per_owner), 1) == l, means[l], mean)
    mean_out[...] = mean

    own = pl.ds(pl.multiple_of(z * rows, rows), rows)
    s8 = place[2:3, own].astype(I32)
    pos = place[1:2, own].astype(I32)
    hot = jnp.where(iota((n * 8, rows), 0) == s8, 1.0, 0.0)
    for c in backs:
        c.wait_recv()
    flat = table[...].reshape(n * 8, CAP).T
    got = jnp.dot(flat, hot, preferred_element_type=F32, precision=lax.Precision.HIGHEST)
    out = jnp.sum(jnp.where(iota((CAP, rows), 0) == pos, got, 0.0), axis=0, keepdims=True)
    best_out[...] = out
    keep_out[...] = jnp.where(out < CUTOFF, 1, 0)
    for group_of in [metas, orders, halves, backs] + lines + planes:
        for c in group_of:
            c.wait_send()


def body(embeddings, cluster_id, member_order, cluster_slot, cluster_size):
    n = lax.axis_size("dev")
    nz, nq = split_lines(n)
    rows, depth = embeddings.shape
    clusters = cluster_slot.shape[0]
    per_owner = clusters // n
    width = min(CHUNK, depth // nz)
    chunks = depth // nz // width
    group, seg = nz * per_owner, CAP // nq
    vmem = pl.BlockSpec(memory_space=pltpu.VMEM)
    dma = pltpu.SemaphoreType.DMA
    best, keep, mean = pl.pallas_call(
        functools.partial(kernel, n, nz, nq),
        out_shape=(jax.ShapeDtypeStruct((1, rows), F32), jax.ShapeDtypeStruct((1, rows), I32),
                   jax.ShapeDtypeStruct((1, per_owner), F32)),
        in_specs=[vmem] * 5,
        out_specs=(vmem,) * 3,
        scratch_shapes=[
            pltpu.VMEM((nz, chunks, rows, width), BF16),
            pltpu.VMEM((chunks, nz, rows, width), BF16),
            pltpu.VMEM((nz, 8, rows), I32),
            pltpu.VMEM((8, nz * rows), F32),
            pltpu.VMEM((nq, group * seg, nz * rows), BF16),
            pltpu.VMEM((chunks, nq, group, seg, width), BF16),
            pltpu.VMEM((chunks, nq, group, seg, width), BF16),
            pltpu.VMEM((nq, 8, CAP), F32),
            pltpu.VMEM((nq, 8, CAP), F32),
            pltpu.VMEM((group, CAP, CAP), F32),
            pltpu.VMEM((nz, per_owner, CAP // 2, CAP), F32),
            pltpu.VMEM((nz, per_owner, CAP // 2, CAP), F32),
            pltpu.VMEM((n, 8, CAP), F32),
            dma((nz,)), dma((nz,)),
            dma((chunks, nz)), dma((chunks, nz)),
            dma((chunks, nq)), dma((chunks, nq)),
            dma((nq,)), dma((nq,)),
            dma((nz,)), dma((nz,)),
            dma((n,)), dma((n,)),
        ],
        compiler_params=pltpu.CompilerParams(
            collective_id=0, has_side_effects=True, vmem_limit_bytes=60 * 1024 * 1024),
    )(embeddings, cluster_id.reshape(1, rows), member_order.reshape(1, rows),
      cluster_slot.reshape(1, clusters), cluster_size.reshape(1, clusters))
    return best.reshape(rows), keep.reshape(rows), mean.reshape(per_owner)


def solution(mesh):
    placed = (P(("rep", "dev"), None), P(("rep", "dev")), P(("rep", "dev")), P("rep"), P("rep"))
    return jax.shard_map(
        body,
        mesh=mesh,
        in_specs=placed,
        out_specs=(P(("rep", "dev")), P(("rep", "dev")), P(("rep", "dev"))),
        check_vma=False,
    )
```

time: 99 us -> 64.2 us (0.65)
  Pallas kernels: 0 us -> 59.9 us
  waiting for transfers between devices: 48.4 us -> 0 us
  starting transfers between devices: 23.2 us -> 0 us
  local copies, waits for them, and re-layouts: 15.8 us -> 3.42 us
  other arithmetic: 6.33 us -> 0 us
  matrix products: 3.99 us -> 0 us
    pallas_call x0 -> x1, Pallas kernels: none -> 59.9 us  [body(): pl.pallas_call(functools.partial(kernel, n, nz, nq), out_shape=(jax.Shape...]
    all_to_all x3 -> x0, waiting for transfers between devices: 48.4 us -> none  [the longest x1 39.6 us: body(): lax.all_to_all(payload, 'dev', split_axis=0, concat_axis=0, tiled=True)]
    all_to_all x3 -> x0, starting transfers between devices: 23.2 us -> none  [the longest x1 9.83 us: body(): lax.all_to_all(answer, 'dev', split_axis=0, concat_axis=0, tiled=True)]
    gather x6 -> x0, local copies, waits for them, and re-layouts: 11.6 us -> none  [the longest x1 3.2 us: body(): payload = normalized(embeddings)[row_pick]]
    dot_general x2 -> x0, matrix products: 3.99 us -> none  [the longest x1 3.02 us: block_best(): jnp.einsum('cid,cjd->cij', row_units, col_units, preferred_element_type=j...]
    unnamed x10 -> x3, local copies, waits for them, and re-layouts: 0.03 us -> 3.42 us
    reduce_sum x4 -> x0, other arithmetic: 2.88 us -> none  [the longest x1 1.82 us: normalized(): squares_sum = jnp.sum(values * values, axis=1, keepdims=True)]
    scatter x2 -> x0, local copies, waits for them, and re-layouts: 2.37 us -> none  [the longest x1 1.4 us: body(): arrival = jnp.zeros((per_owner * capacity,), jnp.int32).at[position].set(...]
  transfers between devices with their start and end apart: 3 -> 0, of which waited for: 3 -> 0; matrix products, arithmetic and copies ran while one was open for 9% -> 0% of each run, Pallas kernels for 0% -> 0%
where the time goes in v1:
time: 64.2 us; the launch traced here: 64 us
  Pallas kernels  59.9 us (93%)
  local copies, waits for them, and re-layouts  3.42 us (5%)
    pallas_call x1, Pallas kernels, body(): pl.pallas_call(functools.partial(kernel, n, nz, nq), out_shape=(jax.Shape...  59.9 us
    unnamed x3, local copies, waits for them, and re-layouts  3.42 us

profile of v1, /device:TPU:0, one launch (start us, length us, event | category | flops | bytes accessed | tf_op | source)
XLA Modules:
  0.0 64.0 jit_solution(6206770063219335126)
XLA Ops:
  0.6 59.9 %shard_map.76 = (f32[1,128]{1,0:T(1,128)}, s32[1,128]{1,0:T(1,128)}, f32[1,2]{1,0:T(1,128)}) custom-call(f32[128,4096]{1,0:T(8,128)} %emb.1, s32[1,128]{1,0:T(1,128)} %bitcast.7, s32[1,128]{1,0:T(1,128)} %bitcast.8, s32[1,32]{1,0:T(1,128)} %bitcast.9, s32[1,32]{1,0:T(1,128)} %bitcast.10), custom_call_target="tpu_custom_call" | custom-call | tf_op jit(solution)/shard_map/pallas_call | solution.py:258
  60.6 1.1 %copy.11 = f32[128]{0:T(128)} copy(f32[128]{0:T(128)} %bitcast.13) | data formatting | bytes 1024
  61.7 1.1 %copy.12 = s32[128]{0:T(128)} copy(s32[128]{0:T(128)} %bitcast.12) | data formatting | bytes 1024
  62.8 1.2 %copy.13 = f32[2]{0:T(128)} copy(f32[2]{0:T(128)} %bitcast.11) | data formatting | bytes 16

commit v2 on v1

--- a/solution.py
+++ b/solution.py
@@ -8,7 +8,9 @@
 from jax.sharding import PartitionSpec as P
 
 CAP = 128
-CHUNK = 256
+CHUNK = 128
+LOADS = 4
+LAG = 2
 NORM_EPS = 1e-06
 CUTOFF = 0.8
 F32 = jnp.float32
@@ -43,10 +45,16 @@
     return jnp.floor((x + 0.5) * (1.0 / d))
 
 
-def kernel(n, nz, nq, emb, cid, order, slot, size, best_out, keep_out, mean_out,
-           unit, line, meta, place, pick, packed, plane, ots, otr, gram, hs, hr, table,
+def kernel(n, nz, nq, emb_hbm, cid, order, slot, size, packed_out,
+           emb, s_load, unit, line, meta, place, pick, packed, plane, ots, otr, gram, hs, hr, table,
            s_meta, r_meta, s_line, r_line, s_plane, r_plane, s_ot, r_ot, s_h, r_h, s_t, r_t):
     me = lax.axis_index("dev")
+    parts = s_load.shape[0]
+    tall = emb.shape[0] // parts
+    loads = [pltpu.make_async_copy(emb_hbm.at[pl.ds(i * tall, tall)], emb.at[pl.ds(i * tall, tall)],
+                                   s_load.at[i]) for i in range(parts)]
+    for c in loads:
+        c.start()
     z, q = lax.div(me, nq), lax.rem(me, nq)
     rows = emb.shape[0]
     clusters = slot.shape[1]
@@ -74,11 +82,14 @@
                             device_id_type=pl.DeviceIdType.MESH)
 
     meta[z] = rows_of([cid[...], order[...]], rows)
-    x = emb[...]
-    scale = lax.rsqrt(jnp.sum(x * x, axis=1, keepdims=True) + NORM_EPS)
+    sums = []
+    for i in range(parts):
+        loads[i].wait()
+        x = emb[i * tall:(i + 1) * tall, :]
+        sums.append(jnp.sum(x * x, axis=1, keepdims=True))
+    scale = lax.rsqrt(jnp.concatenate(sums, axis=0) + NORM_EPS)
     pl.semaphore_wait(barrier, n - 1)
 
-    started = []
     metas = [copy(meta.at[z], meta.at[z], s_meta.at[d], r_meta.at[d], on_line(d) * nq + q)
              for d in range(1, nz)]
     for c in metas:
@@ -89,7 +100,7 @@
             c0 = (t * chunks + k) * width
             unit[t, k] = (emb[:, c0:c0 + width] * scale).astype(BF16)
         now = [copy(unit.at[on_line(d), k], line.at[k, z], s_line.at[k, d], r_line.at[k, d],
-                    on_line(d) * nq + q) for d in range(1, nz)]
+                    on_line(d) * nq + q) for d in range(nz - 1, 0, -1)]
         for c in now:
             c.start()
         line[k, z] = unit[z, k]
@@ -102,7 +113,7 @@
     oz_c = floor_div(owner_c, nq)
     oq_c = owner_c - oz_c * nq
     place_c = oq_c * slots + (oz_c * per_owner + local_c) * seg
-    s8_c = owner_c * 8 + local_c
+    s8_c = slot_c
     for c in metas:
         c.wait_recv()
     tri = (iota((rows, rows), 0) < iota((rows, rows), 1)).astype(F32).astype(BF16)
@@ -131,7 +142,7 @@
         pick[t] = jnp.where(hit, 1.0, 0.0).astype(BF16)
         rows_l = []
         for l in range(per_owner):
-            at = ((z * nq + t) * 8 + l) * CAP
+            at = ((z * nq + t) * per_owner + l) * CAP
             sel = jnp.where(iota((CAP, all_rows), 0) + at == key_i, 1.0, 0.0).astype(BF16)
             r = lax.dot_general(order_b, sel, (((1,), (1,)), ((), ())), preferred_element_type=F32)
             rows_l.append(r[0:1, :])
@@ -144,6 +155,19 @@
               for d in range(1, nq)]
     for c in orders:
         c.start()
+
+    below = iota((half, CAP), 0) + half > iota((half, CAP), 1)
+
+    def partial_gram(k, e):
+        m = plane[k, :, e].reshape(CAP, width)
+        return lax.dot_general(m, m, (((1,), (1,)), ((), ())), preferred_element_type=F32)
+
+    def add_gram(k):
+        for c in planes[k]:
+            c.wait_recv()
+        for e in range(group):
+            s = partial_gram(k, e)
+            gram[e] = s if k == 0 else gram[e] + s
 
     planes = []
     for k in range(chunks):
@@ -164,31 +188,25 @@
                 c.start()
                 now.append(c)
         planes.append(now)
-
-    for k in range(chunks):
-        for c in planes[k]:
-            c.wait_recv()
-        for e in range(group):
-            m = plane[k, :, e].reshape(CAP, width)
-            s = lax.dot_general(m, m, (((1,), (1,)), ((), ())), preferred_element_type=F32)
-            if k == 0:
-                gram[e] = s
-            else:
-                gram[e] = gram[e] + s
-
-    below = iota((half, CAP), 0) + half > iota((half, CAP), 1)
-
-    def pack_half(t, _):
+        if k >= LAG:
+            add_gram(k - LAG)
+
+    for k in range(max(chunks - LAG, 0), chunks - 1):
+        add_gram(k)
+    for c in planes[chunks - 1]:
+        c.wait_recv()
+    halves = []
+    for d in list(range(1, nz)) + [0]:
+        t = on_line(d)
         for l in range(per_owner):
-            full = gram[t * per_owner + l]
+            full = partial_gram(chunks - 1, t * per_owner + l)
+            if chunks > 1:
+                full = full + gram[t * per_owner + l]
             hs[t, l] = jnp.where(below, full[half:, :], pltpu.roll(full[:half, :], half, 1))
-        return 0
-
-    lax.fori_loop(0, nz, pack_half, 0)
-    halves = [copy(hs.at[on_line(d)], hr.at[z], s_h.at[d], r_h.at[d], on_line(d) * nq + q)
-              for d in range(1, nz)]
-    for c in halves:
-        c.start()
+        if d:
+            c = copy(hs.at[t], hr.at[z], s_h.at[d], r_h.at[d], t * nq + q)
+            c.start()
+            halves.append(c)
     hr[z] = hs[z]
     for c in orders:
         c.wait_recv()
@@ -218,30 +236,35 @@
         live = (o_row >= 1.0) & (o_row <= n_mem)
         bests.append(jnp.where(live, near, -1.0))
         means.append(jnp.sum(jnp.where(live, near, 0.0), axis=1, keepdims=True) / n_mem)
-    table[me] = rows_of(bests, CAP)
+    table[me] = jnp.concatenate(bests, axis=0)
     backs = [copy(table.at[me], table.at[me], s_t.at[d], r_t.at[d], lax.rem(me + d, n))
              for d in range(1, n)]
     for c in backs:
         c.start()
-    mean = jnp.zeros((1, per_owner), F32)
+    mean = jnp.zeros((1, rows), F32)
     for l in range(per_owner):
-        mean = jnp.where(iota((1, per_owner), 1) == l, means[l], mean)
-    mean_out[...] = mean
+        mean = jnp.where(iota((1, rows), 1) == l, means[l], mean)
 
     own = pl.ds(pl.multiple_of(z * rows, rows), rows)
     s8 = place[2:3, own].astype(I32)
     pos = place[1:2, own].astype(I32)
-    hot = jnp.where(iota((n * 8, rows), 0) == s8, 1.0, 0.0)
+    hot = jnp.where(iota((clusters, rows), 0) == s8, 1.0, 0.0)
     for c in backs:
         c.wait_recv()
-    flat = table[...].reshape(n * 8, CAP).T
+    flat = table[...].reshape(clusters, CAP).T
     got = jnp.dot(flat, hot, preferred_element_type=F32, precision=lax.Precision.HIGHEST)
     out = jnp.sum(jnp.where(iota((CAP, rows), 0) == pos, got, 0.0), axis=0, keepdims=True)
-    best_out[...] = out
-    keep_out[...] = jnp.where(out < CUTOFF, 1, 0)
+    packed_out[...] = rows_of([out, mean], rows)
     for group_of in [metas, orders, halves, backs] + lines + planes:
         for c in group_of:
             c.wait_send()
+
+
+def finish(packed, best_out, keep_out, mean_out):
+    best = packed[0:1, :]
+    best_out[...] = best
+    keep_out[...] = jnp.where(best < CUTOFF, 1, 0)
+    mean_out[...] = packed[1:2, :mean_out.shape[1]]
 
 
 def body(embeddings, cluster_id, member_order, cluster_slot, cluster_size):
@@ -255,13 +278,14 @@
     group, seg = nz * per_owner, CAP // nq
     vmem = pl.BlockSpec(memory_space=pltpu.VMEM)
     dma = pltpu.SemaphoreType.DMA
-    best, keep, mean = pl.pallas_call(
+    packed = pl.pallas_call(
         functools.partial(kernel, n, nz, nq),
-        out_shape=(jax.ShapeDtypeStruct((1, rows), F32), jax.ShapeDtypeStruct((1, rows), I32),
-                   jax.ShapeDtypeStruct((1, per_owner), F32)),
-        in_specs=[vmem] * 5,
-        out_specs=(vmem,) * 3,
+        out_shape=jax.ShapeDtypeStruct((8, rows), F32),
+        in_specs=[pl.BlockSpec(memory_space=pl.ANY)] + [vmem] * 4,
+        out_specs=vmem,
         scratch_shapes=[
+            pltpu.VMEM((rows, depth), F32),
+            dma((LOADS,)),
             pltpu.VMEM((nz, chunks, rows, width), BF16),
             pltpu.VMEM((chunks, nz, rows, width), BF16),
             pltpu.VMEM((nz, 8, rows), I32),
@@ -274,7 +298,7 @@
             pltpu.VMEM((group, CAP, CAP), F32),
             pltpu.VMEM((nz, per_owner, CAP // 2, CAP), F32),
             pltpu.VMEM((nz, per_owner, CAP // 2, CAP), F32),
-            pltpu.VMEM((n, 8, CAP), F32),
+            pltpu.VMEM((n, per_owner, CAP), F32),
             dma((nz,)), dma((nz,)),
             dma((chunks, nz)), dma((chunks, nz)),
             dma((chunks, nq)), dma((chunks, nq)),
@@ -286,6 +310,13 @@
             collective_id=0, has_side_effects=True, vmem_limit_bytes=60 * 1024 * 1024),
     )(embeddings, cluster_id.reshape(1, rows), member_order.reshape(1, rows),
       cluster_slot.reshape(1, clusters), cluster_size.reshape(1, clusters))
+    best, keep, mean = pl.pallas_call(
+        finish,
+        out_shape=(jax.ShapeDtypeStruct((1, rows), F32), jax.ShapeDtypeStruct((1, rows), I32),
+                   jax.ShapeDtypeStruct((1, per_owner), F32)),
+        in_specs=[vmem],
+        out_specs=(vmem,) * 3,
+    )(packed)
     return best.reshape(rows), keep.reshape(rows), mean.reshape(per_owner)
 
 

time: 64.2 us -> 57.3 us (0.89)
  Pallas kernels: 59.9 us -> 56.4 us
  local copies, waits for them, and re-layouts: 3.42 us -> 0 us
    pallas_call x1 -> x2, Pallas kernels: 59.9 us -> 56.4 us  [the longest x1 55.2 us: body(): pl.pallas_call(functools.partial(kernel, n, nz, nq), out_shape=jax.ShapeD...]
    unnamed x3 -> x0, local copies, waits for them, and re-layouts: 3.42 us -> none
where the time goes in v2:
time: 57.3 us; the launch traced here: 57.1 us
  Pallas kernels  56.4 us (98%)
  between operations  0.64 us (1%)
    pallas_call x1, Pallas kernels, body(): pl.pallas_call(functools.partial(kernel, n, nz, nq), out_shape=jax.ShapeD...  55.2 us
    pallas_call x1, Pallas kernels, body(): pl.pallas_call(finish, out_shape=(jax.ShapeDtypeStruct((1, rows), F32), j...  1.19 us

profile of v2, /device:TPU:0, one launch (start us, length us, event | category | flops | bytes accessed | tf_op | source)
XLA Modules:
  0.0 57.1 jit_solution(6224547302183475078)
XLA Ops:
  0.6 55.2 %shard_map.76.packed = f32[8,128]{1,0:T(8,128)} custom-call(f32[128,4096]{1,0:T(8,128)} %emb_hbm.1, s32[1,128]{1,0:T(1,128)} %bitcast.7, s32[1,128]{1,0:T(1,128)} %bitcast.8, s32[1,32]{1,0:T(1,128)} %bitcast.9, s32[1,32]{1,0:T(1,128)} %bitcast.10), custom_call_target="tpu_custom_call" | custom-call | tf_op jit(solution)/shard_map/pallas_call | solution.py:281
  55.9 1.2 %shard_map.77 = (f32[1,128]{1,0:T(1,128)}, s32[1,128]{1,0:T(1,128)}, f32[1,2]{1,0:T(1,128)}) custom-call(f32[8,128]{1,0:T(8,128)} %shard_map.76.packed), custom_call_target="tpu_custom_call" | custom-call | tf_op jit(solution)/shard_map/pallas_call | solution.py:313

commit v3 on v2

--- a/solution.py
+++ b/solution.py
@@ -77,8 +77,9 @@
         return lax.rem(q + d, nq)
 
     barrier = pltpu.get_barrier_semaphore()
-    for d in range(1, n):
-        pl.semaphore_signal(barrier, inc=1, device_id={"dev": lax.rem(me + d, n)},
+    friends = [on_line(d) * nq + q for d in range(1, nz)] + [z * nq + on_plane(d) for d in range(1, nq)]
+    for t in friends:
+        pl.semaphore_signal(barrier, inc=1, device_id={"dev": t},
                             device_id_type=pl.DeviceIdType.MESH)
 
     meta[z] = rows_of([cid[...], order[...]], rows)
@@ -88,7 +89,7 @@
         x = emb[i * tall:(i + 1) * tall, :]
         sums.append(jnp.sum(x * x, axis=1, keepdims=True))
     scale = lax.rsqrt(jnp.concatenate(sums, axis=0) + NORM_EPS)
-    pl.semaphore_wait(barrier, n - 1)
+    pl.semaphore_wait(barrier, len(friends))
 
     metas = [copy(meta.at[z], meta.at[z], s_meta.at[d], r_meta.at[d], on_line(d) * nq + q)
              for d in range(1, nz)]

time: 57.3 us -> 55.2 us (0.963)
  Pallas kernels: 56.4 us -> 54.3 us
    pallas_call x1, Pallas kernels: 55.2 us -> 53.1 us  [body(): pl.pallas_call(functools.partial(kernel, n, nz, nq), out_shape=jax.ShapeD...]
where the time goes in v3:
time: 55.2 us; the launch traced here: 55 us
  Pallas kernels  54.3 us (98%)
  between operations  0.64 us (1%)
    pallas_call x1, Pallas kernels, body(): pl.pallas_call(functools.partial(kernel, n, nz, nq), out_shape=jax.ShapeD...  53.1 us
    pallas_call x1, Pallas kernels, body(): pl.pallas_call(finish, out_shape=(jax.ShapeDtypeStruct((1, rows), F32), j...  1.19 us

profile of v3, /device:TPU:0, one launch (start us, length us, event | category | flops | bytes accessed | tf_op | source)
XLA Modules:
  0.0 55.0 jit_solution(16995564315878948211)
XLA Ops:
  0.6 53.1 %shard_map.76.packed = f32[8,128]{1,0:T(8,128)} custom-call(f32[128,4096]{1,0:T(8,128)} %emb_hbm.1, s32[1,128]{1,0:T(1,128)} %bitcast.7, s32[1,128]{1,0:T(1,128)} %bitcast.8, s32[1,32]{1,0:T(1,128)} %bitcast.9, s32[1,32]{1,0:T(1,128)} %bitcast.10), custom_call_target="tpu_custom_call" | custom-call | tf_op jit(solution)/shard_map/pallas_call | solution.py:282
  53.8 1.2 %shard_map.77 = (f32[1,128]{1,0:T(1,128)}, s32[1,128]{1,0:T(1,128)}, f32[1,2]{1,0:T(1,128)}) custom-call(f32[8,128]{1,0:T(8,128)} %shard_map.76.packed), custom_call_target="tpu_custom_call" | custom-call | tf_op jit(solution)/shard_map/pallas_call | solution.py:314

commit v4 on v3

--- a/solution.py
+++ b/solution.py
@@ -19,9 +19,14 @@
 
 
 def split_lines(n):
-    for z in range(1, n + 1):
-        if n % z == 0 and z * z >= n:
-            return z, n // z
+    z = max(z for z in range(1, n + 1) if n % z == 0 and z * z <= n)
+    return z, n // z
+
+
+def line_slots(n, nz, nq, rows, group):
+    largest = rows * n // nq + CAP - CAP // nq
+    bound = -(-largest // nq) + -(-group * nz * (n - 1) // n)
+    return min(group * (CAP // nq), -(-bound // 16) * 16)
 
 
 def iota(shape, dim):
@@ -46,7 +51,7 @@
 
 
 def kernel(n, nz, nq, emb_hbm, cid, order, slot, size, packed_out,
-           emb, s_load, unit, line, meta, place, pick, packed, plane, ots, otr, gram, hs, hr, table,
+           emb, s_load, unit, line, meta, place, pick, packed, plane, ots, otr, gram, hs, hr, table, units, repack, labs,
            s_meta, r_meta, s_line, r_line, s_plane, r_plane, s_ot, r_ot, s_h, r_h, s_t, r_t):
     me = lax.axis_index("dev")
     parts = s_load.shape[0]
@@ -62,7 +67,7 @@
     chunks, width = unit.shape[1], unit.shape[3]
     group = nz * per_owner
     seg = CAP // nq
-    slots = group * seg
+    slots = pick.shape[1]
     half = CAP // 2
 
     def copy(src, dst, s, r, target):
@@ -109,15 +114,30 @@
 
     slot_c = to_col(slot[...].astype(F32), clusters)
     size_c = to_col(size[...].astype(F32), clusters)
-    owner_c = floor_div(slot_c, per_owner)
-    local_c = slot_c - owner_c * per_owner
-    oz_c = floor_div(owner_c, nq)
-    oq_c = owner_c - oz_c * nq
-    place_c = oq_c * slots + (oz_c * per_owner + local_c) * seg
-    s8_c = slot_c
+    size_r = size[...].astype(F32)
+    c_row, c_col = iota((clusters, clusters), 1), iota((clusters, clusters), 0)
+    ahead = (size_r > size_c) | ((size_r == size_c) & (c_row < c_col))
+    place_in = jnp.sum(jnp.where(ahead, 1.0, 0.0), axis=1, keepdims=True)
+    e_c = floor_div(place_in, nq)
+    turn = place_in - e_c * nq
+    odd = e_c - 2.0 * floor_div(e_c, 2)
+    g_c = jnp.where(odd > 0.5, nq - 1 - turn, turn)
+    oz_c = floor_div(e_c, per_owner)
+    local_c = e_c - oz_c * per_owner
+    work_c = (oz_c * nq + g_c) * per_owner + local_c
     for c in metas:
         c.wait_recv()
     tri = (iota((rows, rows), 0) < iota((rows, rows), 1)).astype(F32).astype(BF16)
+    counts = jnp.zeros((clusters, 1), F32)
+    for b in range(nz):
+        mem = jnp.where(iota((clusters, rows), 0) == meta[b, 0:1, :], 1.0, 0.0)
+        counts = counts + jnp.sum(mem, axis=1, keepdims=True)
+    eye = c_row == c_col
+    g_r = jnp.sum(jnp.where(eye, g_c, 0.0), axis=0, keepdims=True)
+    e_r = jnp.sum(jnp.where(eye, e_c, 0.0), axis=0, keepdims=True)
+    n_r = jnp.sum(jnp.where(eye, counts, 0.0), axis=0, keepdims=True)
+    first = (g_r == g_c) & (e_r < e_c)
+    place_c = g_c * slots + jnp.sum(jnp.where(first, n_r, 0.0), axis=1, keepdims=True)
     base = jnp.zeros((clusters, 1), F32)
     for b in range(nz):
         is_mem = iota((clusters, rows), 0) == meta[b, 0:1, :]
@@ -128,26 +148,22 @@
             return jnp.sum(jnp.where(is_mem, v, 0.0), axis=0, keepdims=True)
 
         rank = of_row(before)
-        vals = [of_row(place_c) + rank, rank + (q * seg).astype(F32), of_row(s8_c),
-                meta[b, 1:2, :].astype(F32) + 1.0]
+        vals = [of_row(place_c) + rank, rank + (q * seg).astype(F32), of_row(work_c),
+                meta[b, 1:2, :].astype(F32) + 1.0, of_row(e_c) + 1.0]
         place[:, b * rows:(b + 1) * rows] = rows_of(vals, rows)
         base = base + jnp.sum(mem, axis=1, keepdims=True)
 
     all_rows = nz * rows
     place_i = place[0:1, :].astype(I32)
-    key_i = (place[2:3, :] * CAP + place[1:2, :]).astype(I32)
-    order_b = jnp.broadcast_to(place[3:4, :], (8, all_rows)).astype(BF16)
+    label_row = iota((8, all_rows), 0)
+    small = (label_row == 1) | (label_row == 3) | (label_row == 4)
+    labels = jnp.where(small, place[...], 0.0).astype(BF16)
 
     def make_pick(t, _):
         hit = iota((slots, all_rows), 0) + t * slots == place_i
         pick[t] = jnp.where(hit, 1.0, 0.0).astype(BF16)
-        rows_l = []
-        for l in range(per_owner):
-            at = ((z * nq + t) * per_owner + l) * CAP
-            sel = jnp.where(iota((CAP, all_rows), 0) + at == key_i, 1.0, 0.0).astype(BF16)
-            r = lax.dot_general(order_b, sel, (((1,), (1,)), ((), ())), preferred_element_type=F32)
-            rows_l.append(r[0:1, :])
-        ots[t] = rows_of(rows_l, CAP)
+        ots[t] = lax.dot_general(labels, pick[t], (((1,), (1,)), ((), ())),
+                                 preferred_element_type=F32)
         return 0
 
     lax.fori_loop(0, nq, make_pick, 0)
@@ -159,16 +175,38 @@
 
     below = iota((half, CAP), 0) + half > iota((half, CAP), 1)
 
-    def partial_gram(k, e):
-        m = plane[k, :, e].reshape(CAP, width)
-        return lax.dot_general(m, m, (((1,), (1,)), ((), ())), preferred_element_type=F32)
-
-    def add_gram(k):
+    def spread(k):
         for c in planes[k]:
             c.wait_recv()
+        got = jnp.dot(repack[...].reshape(group * CAP, nq * slots),
+                      plane[k].reshape(nq * slots, width), preferred_element_type=F32)
+        units[...] = got.astype(BF16).reshape(group, CAP, width)
+
+    def partial_gram(e):
+        m = units[e]
+        return lax.dot_general(m, m, (((1,), (1,)), ((), ())), preferred_element_type=F32)
+
+    def add_gram(k):
+        if k == 0:
+            make_repack()
+        spread(k)
         for e in range(group):
-            s = partial_gram(k, e)
+            s = partial_gram(e)
             gram[e] = s if k == 0 else gram[e] + s
+
+    def make_repack():
+        for c in orders:
+            c.wait_recv()
+        for t in range(nq):
+            labs[:, t * slots:(t + 1) * slots] = otr[t]
+        target = ((labs[4:5, :] - 1.0) * CAP + labs[1:2, :]).astype(I32)
+
+        def one(e, _):
+            hit = iota((CAP, nq * slots), 0) + e * CAP == target
+            repack[e] = jnp.where(hit, 1.0, 0.0).astype(BF16)
+            return 0
+
+        lax.fori_loop(0, group, one, 0)
 
     planes = []
     for k in range(chunks):
@@ -179,7 +217,6 @@
         for d in list(range(1, nq)) + [0]:
             t = on_plane(d)
             got = jnp.dot(pick[t], block, preferred_element_type=F32).astype(BF16)
-            got = got.reshape(group, seg, width)
             if d == 0:
                 plane[k, q] = got
             else:
@@ -194,13 +231,14 @@
 
     for k in range(max(chunks - LAG, 0), chunks - 1):
         add_gram(k)
-    for c in planes[chunks - 1]:
-        c.wait_recv()
+    if chunks == 1:
+        make_repack()
+    spread(chunks - 1)
     halves = []
     for d in list(range(1, nz)) + [0]:
         t = on_line(d)
         for l in range(per_owner):
-            full = partial_gram(chunks - 1, t * per_owner + l)
+            full = partial_gram(t * per_owner + l)
             if chunks > 1:
                 full = full + gram[t * per_owner + l]
             hs[t, l] = jnp.where(below, full[half:, :], pltpu.roll(full[:half, :], half, 1))
@@ -209,11 +247,13 @@
             c.start()
             halves.append(c)
     hr[z] = hs[z]
-    for c in orders:
-        c.wait_recv()
-    ord_r = otr[0]
-    for t in range(1, nq):
-        ord_r = ord_r + otr[t]
+    ranks = labs[...].astype(BF16)
+    ord_rows = []
+    for l in range(per_owner):
+        r = lax.dot_general(ranks, repack[z * per_owner + l], (((1,), (1,)), ((), ())),
+                            preferred_element_type=F32)
+        ord_rows.append(r[3:4, :])
+    ord_r = rows_of(ord_rows, CAP)
     ord_cols = ord_r.T
     for c in halves:
         c.wait_recv()
@@ -230,29 +270,38 @@
         bottom = jnp.concatenate([p[:, :half], jnp.where(down, u, ut)], axis=1)
         sim = jnp.concatenate([top, bottom], axis=0)
         mine = (me * per_owner + l).astype(F32)
-        n_mem = jnp.sum(jnp.where(slot_c == mine, size_c, 0.0), axis=0, keepdims=True)
+        n_mem = jnp.sum(jnp.where(work_c == mine, size_c, 0.0), axis=0, keepdims=True)
         o_row, o_col = ord_r[l:l + 1, :], ord_cols[:, l:l + 1]
         ok = (o_col < o_row) & (o_col >= 1.0) & (o_col <= n_mem)
         near = jnp.max(jnp.where(ok, sim, -1.0), axis=0, keepdims=True)
         live = (o_row >= 1.0) & (o_row <= n_mem)
         bests.append(jnp.where(live, near, -1.0))
         means.append(jnp.sum(jnp.where(live, near, 0.0), axis=1, keepdims=True) / n_mem)
-    table[me] = jnp.concatenate(bests, axis=0)
+    lanes = jnp.zeros((1, CAP), F32)
+    for l in range(per_owner):
+        lanes = jnp.where(iota((1, CAP), 1) == l, means[l], lanes)
+    table[me] = rows_of(bests + [lanes], CAP)
     backs = [copy(table.at[me], table.at[me], s_t.at[d], r_t.at[d], lax.rem(me + d, n))
              for d in range(1, n)]
     for c in backs:
         c.start()
-    mean = jnp.zeros((1, rows), F32)
-    for l in range(per_owner):
-        mean = jnp.where(iota((1, rows), 1) == l, means[l], mean)
-
     own = pl.ds(pl.multiple_of(z * rows, rows), rows)
     s8 = place[2:3, own].astype(I32)
     pos = place[1:2, own].astype(I32)
     hot = jnp.where(iota((clusters, rows), 0) == s8, 1.0, 0.0)
     for c in backs:
         c.wait_recv()
-    flat = table[...].reshape(clusters, CAP).T
+    full = table[...]
+    flat = full[:, :per_owner, :].reshape(clusters, CAP).T
+    told = full[:, per_owner:per_owner + 1, :].reshape(n, CAP)
+    mean = jnp.zeros((1, rows), F32)
+    for l in range(per_owner):
+        own_slot = (me * per_owner + l).astype(F32)
+        work = jnp.sum(jnp.where(slot_c == own_slot, work_c, 0.0), axis=0, keepdims=True).astype(I32)
+        hit = iota((n, CAP), 0) * per_owner + iota((n, CAP), 1) == work
+        hit = hit & (iota((n, CAP), 1) < per_owner)
+        part = jnp.sum(jnp.where(hit, told, 0.0), axis=1, keepdims=True)
+        mean = jnp.where(iota((1, rows), 1) == l, jnp.sum(part, axis=0, keepdims=True), mean)
     got = jnp.dot(flat, hot, preferred_element_type=F32, precision=lax.Precision.HIGHEST)
     out = jnp.sum(jnp.where(iota((CAP, rows), 0) == pos, got, 0.0), axis=0, keepdims=True)
     packed_out[...] = rows_of([out, mean], rows)
@@ -276,7 +325,8 @@
     per_owner = clusters // n
     width = min(CHUNK, depth // nz)
     chunks = depth // nz // width
-    group, seg = nz * per_owner, CAP // nq
+    group = nz * per_owner
+    slots = line_slots(n, nz, nq, rows, group)
     vmem = pl.BlockSpec(memory_space=pltpu.VMEM)
     dma = pltpu.SemaphoreType.DMA
     packed = pl.pallas_call(
@@ -291,15 +341,18 @@
             pltpu.VMEM((chunks, nz, rows, width), BF16),
             pltpu.VMEM((nz, 8, rows), I32),
             pltpu.VMEM((8, nz * rows), F32),
-            pltpu.VMEM((nq, group * seg, nz * rows), BF16),
-            pltpu.VMEM((chunks, nq, group, seg, width), BF16),
-            pltpu.VMEM((chunks, nq, group, seg, width), BF16),
-            pltpu.VMEM((nq, 8, CAP), F32),
-            pltpu.VMEM((nq, 8, CAP), F32),
+            pltpu.VMEM((nq, slots, nz * rows), BF16),
+            pltpu.VMEM((chunks, nq, slots, width), BF16),
+            pltpu.VMEM((chunks, nq, slots, width), BF16),
+            pltpu.VMEM((nq, 8, slots), F32),
+            pltpu.VMEM((nq, 8, slots), F32),
             pltpu.VMEM((group, CAP, CAP), F32),
             pltpu.VMEM((nz, per_owner, CAP // 2, CAP), F32),
             pltpu.VMEM((nz, per_owner, CAP // 2, CAP), F32),
-            pltpu.VMEM((n, per_owner, CAP), F32),
+            pltpu.VMEM((n, 8, CAP), F32),
+            pltpu.VMEM((group, CAP, width), BF16),
+            pltpu.VMEM((group, CAP, nq * slots), BF16),
+            pltpu.VMEM((8, nq * slots), F32),
             dma((nz,)), dma((nz,)),
             dma((chunks, nz)), dma((chunks, nz)),
             dma((chunks, nq)), dma((chunks, nq)),

time: 55.2 us -> 54.6 us (0.989)
  Pallas kernels: 54.3 us -> 53.7 us
    pallas_call x1, Pallas kernels: 53.1 us -> 52.5 us  [body(): pl.pallas_call(functools.partial(kernel, n, nz, nq), out_shape=jax.ShapeD...]
where the time goes in v4:
time: 54.6 us; the launch traced here: 54.4 us
  Pallas kernels  53.7 us (98%)
  between operations  0.64 us (1%)
    pallas_call x1, Pallas kernels, body(): pl.pallas_call(functools.partial(kernel, n, nz, nq), out_shape=jax.ShapeD...  52.5 us
    pallas_call x1, Pallas kernels, body(): pl.pallas_call(finish, out_shape=(jax.ShapeDtypeStruct((1, rows), F32), j...  1.19 us

profile of v4, /device:TPU:0, one launch (start us, length us, event | category | flops | bytes accessed | tf_op | source)
XLA Modules:
  0.0 54.4 jit_solution(6193363074950241495)
XLA Ops:
  0.6 52.5 %shard_map.76.packed = f32[8,128]{1,0:T(8,128)} custom-call(f32[128,4096]{1,0:T(8,128)} %emb_hbm.1, s32[1,128]{1,0:T(1,128)} %bitcast.7, s32[1,128]{1,0:T(1,128)} %bitcast.8, s32[1,32]{1,0:T(1,128)} %bitcast.9, s32[1,32]{1,0:T(1,128)} %bitcast.10), custom_call_target="tpu_custom_call" | custom-call | tf_op jit(solution)/shard_map/pallas_call | solution.py:332
  53.2 1.2 %shard_map.77 = (f32[1,128]{1,0:T(1,128)}, s32[1,128]{1,0:T(1,128)}, f32[1,2]{1,0:T(1,128)}) custom-call(f32[8,128]{1,0:T(8,128)} %shard_map.76.packed), custom_call_target="tpu_custom_call" | custom-call | tf_op jit(solution)/shard_map/pallas_call | solution.py:367

commit v5 on v4

--- a/solution.py
+++ b/solution.py
@@ -280,7 +280,7 @@
     lanes = jnp.zeros((1, CAP), F32)
     for l in range(per_owner):
         lanes = jnp.where(iota((1, CAP), 1) == l, means[l], lanes)
-    table[me] = rows_of(bests + [lanes], CAP)
+    table[me] = rows_of(bests + [lanes], CAP)[:table.shape[1], :]
     backs = [copy(table.at[me], table.at[me], s_t.at[d], r_t.at[d], lax.rem(me + d, n))
              for d in range(1, n)]
     for c in backs:
@@ -349,7 +349,7 @@
             pltpu.VMEM((group, CAP, CAP), F32),
             pltpu.VMEM((nz, per_owner, CAP // 2, CAP), F32),
             pltpu.VMEM((nz, per_owner, CAP // 2, CAP), F32),
-            pltpu.VMEM((n, 8, CAP), F32),
+            pltpu.VMEM((n, pl.next_power_of_2(per_owner + 1), CAP), F32),
             pltpu.VMEM((group, CAP, width), BF16),
             pltpu.VMEM((group, CAP, nq * slots), BF16),
             pltpu.VMEM((8, nq * slots), F32),

time: 54.6 us -> 54.3 us (level)
  no operation moved by 1% of the time
where the time goes in v5:
time: 54.3 us; the launch traced here: 54.1 us
  Pallas kernels  53.5 us (99%)
  between operations  0.64 us (1%)
    pallas_call x1, Pallas kernels, body(): pl.pallas_call(functools.partial(kernel, n, nz, nq), out_shape=jax.ShapeD...  52.3 us
    pallas_call x1, Pallas kernels, body(): pl.pallas_call(finish, out_shape=(jax.ShapeDtypeStruct((1, rows), F32), j...  1.19 us

profile of v5, /device:TPU:0, one launch (start us, length us, event | category | flops | bytes accessed | tf_op | source)
XLA Modules:
  0.0 54.1 jit_solution(11651562035436768208)
XLA Ops:
  0.6 52.3 %shard_map.76.packed = f32[8,128]{1,0:T(8,128)} custom-call(f32[128,4096]{1,0:T(8,128)} %emb_hbm.1, s32[1,128]{1,0:T(1,128)} %bitcast.7, s32[1,128]{1,0:T(1,128)} %bitcast.8, s32[1,32]{1,0:T(1,128)} %bitcast.9, s32[1,32]{1,0:T(1,128)} %bitcast.10), custom_call_target="tpu_custom_call" | custom-call | tf_op jit(solution)/shard_map/pallas_call | solution.py:332
  52.9 1.2 %shard_map.77 = (f32[1,128]{1,0:T(1,128)}, s32[1,128]{1,0:T(1,128)}, f32[1,2]{1,0:T(1,128)}) custom-call(f32[8,128]{1,0:T(8,128)} %shard_map.76.packed), custom_call_target="tpu_custom_call" | custom-call | tf_op jit(solution)/shard_map/pallas_call | solution.py:367
